TPU v7x, 128 devices: a whole 4x4x4 slice. The times are simulated.
128 devices in a mesh: seq: 32 (over y, z, core), dp: 4 (over x).
Axes of the slice: x: 4, y: 4, z: 4, core: 2. Of those that a mesh axis runs over, the one named last changes fastest.
Arguments:
- attention_queries: bfloat16 [32, 2, 256, 4096], P('seq', None, 'dp'), parts along dimension 2, may hold values from -5.5 to 5.5
- attention_keys: bfloat16 [32, 2, 256, 512], P('seq', None, 'dp'), parts along dimension 2, may hold values from -7.5 to 7.5
- attention_values: bfloat16 [32, 2, 256, 512], P('seq', None, 'dp'), parts along dimension 2, may hold values from -6 to 6
- attention_output: bfloat16 [32, 2, 256, 4096], P('seq', None, 'dp'), parts along dimension 2, may hold values from -6 to 6
- output_gradient: bfloat16 [32, 2, 256, 4096], P('seq', None, 'dp'), parts along dimension 2, may hold values from -48 to 48
- logsumexp_rows: float32 [32, 2, 256, 32], P('seq', None, 'dp'), parts along dimension 2, as said below
Outputs:
- grad_query: float32 [32, 2, 256, 4096], P('seq', None, 'dp'), parts along dimension 2
- key_gradient: float32 [32, 2, 256, 512], P('seq', None, 'dp'), parts along dimension 2
- value_gradient: float32 [32, 2, 256, 512], P('seq', None, 'dp'), parts along dimension 2
There are 4 independent parts, one for each index of `dp`. A program takes and returns all parts, laid end to end along the dimension named above; each array names one. Nothing has to cross between parts.
Inputs may be any that keep to these rules, and one draw needn't show every extreme that they name: logsumexp_rows[i, h] is the logarithm of the sum over key positions t <= i of exp(scores[h, i, t]), computed from attention_queries and attention_keys in float32.
All inputs are finite; a program needn't handle non-finite values.
Results may differ from a plain program's by a relative error of at most 0.0003.
Values may be sent and summed in bfloat16 or wider, within the bound.
No kernel may reach another device: no remote copies, remote signals or barrier semaphores. Data moves between devices by JAX's collectives and lax.ppermute only.
A program may use at most 128 MiB of HBM per device.

v0:
```python
import jax
import jax.numpy as jnp
from jax import lax
from jax.experimental import pallas as pl
from jax.experimental.pallas import tpu as pltpu
from jax.sharding import PartitionSpec as P

HEAD = 128
GROUP = 8
BLOCK = 64
ROWS = GROUP * BLOCK
WIDTH = GROUP * HEAD
HEADS = 4
TILE = 512
VMEM_LIMIT = 28 * 2**20
HALF = 32 * BLOCK
STEPS = (0, 1, 3, 2)
SCALE = HEAD ** -0.5
LOG2E = 1.4426950408889634
F32 = jnp.float32
BF16 = jnp.bfloat16


def along_y(step):
    return [(i, (i + 8 * step) % 32) for i in range(32)]


def along_z(step):
    return [(i, (i // 8) * 8 + (i + 2 * step) % 8) for i in range(32)]


OTHER_CORE = [(i, i ^ 1) for i in range(32)]
Y_GROUPS = [[zc + 8 * y for y in range(4)] for zc in range(8)]


def dot(a, b):
    return jnp.dot(a, b, preferred_element_type=F32)


def split(values):
    high = values.astype(BF16)
    return high, (values - high.astype(F32)).astype(BF16)


def owner_of(index, back):
    y, z, c = index // 8, (index // 2) % 4, index % 2
    return ((y + 4 - back) % 4) * 8 + z * 2 + c


def load_block(x_ref, work):
    q_s, do_s, qt_s, dot_s, log_s, delta_s = work
    for j in range(GROUP):
        q_s[j * BLOCK:(j + 1) * BLOCK, :] = x_ref[0, 0:BLOCK, j * HEAD:(j + 1) * HEAD]
        do_s[j * BLOCK:(j + 1) * BLOCK, :] = x_ref[
            0, 0:BLOCK, WIDTH + j * HEAD:WIDTH + (j + 1) * HEAD
        ]
    qt, dt = q_s[...].T, do_s[...].T
    for at in (0, ROWS):
        qt_s[:, at:at + ROWS] = qt
        dot_s[:, at:at + ROWS] = dt
    aux = x_ref[0, :, 2 * WIDTH:].astype(F32)
    aux = aux[:, 0:16] + aux[:, 16:32] + aux[:, 32:48]
    for j in range(GROUP):
        rows = slice(j * BLOCK, (j + 1) * BLOCK)
        log_s[rows, :] = jnp.broadcast_to(aux[:, j:j + 1] * LOG2E, (BLOCK, HEAD))
        delta_s[rows, :] = jnp.broadcast_to(
            aux[:, GROUP + j:GROUP + j + 1], (BLOCK, HEAD)
        )


def sweep(block, low, high, masked, base, kt_ref, vt_ref, dk_ref, dv_ref, dq_s, work, rel_s):
    q_s, do_s, qt_s, dot_s, log_s, delta_s = work
    repeat = TILE // HEAD

    def tile(t, diagonal):
        at = pl.multiple_of(t * TILE - base, TILE)
        keys = pl.ds(at, TILE)
        kt, vt = kt_ref[:, keys], vt_ref[:, keys]
        scores = dot(q_s[...], kt)
        weight_grad = dot(do_s[...], vt)
        log_b = jnp.concatenate([log_s[...]] * repeat, 1)
        delta_b = jnp.concatenate([delta_s[...]] * repeat, 1)
        weights = jnp.exp2(scores * (SCALE * LOG2E) - log_b)
        if diagonal:
            weights = jnp.where(rel_s[...] <= block * BLOCK - t * TILE, weights, 0.0)
        w_high, w_rest = split(weights)
        s_high, s_rest = split(weights * (weight_grad - delta_b))
        dv_ref[:, keys] += dot(dot_s[...], jnp.concatenate([w_high, w_rest], 0))
        dk_ref[:, keys] += dot(qt_s[...], jnp.concatenate([s_high, s_rest], 0))
        dq_s[...] += dot(
            jnp.concatenate([kt, kt], 1), jnp.concatenate([s_high.T, s_rest.T], 0)
        )

    @pl.loop(low, high)
    def _(t):
        tile(t, False)

    if masked is True:
        tile(high, True)
    elif masked is not False:
        @pl.when(masked)
        def _():
            tile(high, True)


def relative(rel_s):
    shape = (ROWS, TILE)
    rel_s[...] = lax.broadcasted_iota(jnp.int32, shape, 1) - (
        lax.broadcasted_iota(jnp.int32, shape, 0) % BLOCK
    )


def write_queries(dq_s, dq_ref):
    dq = (dq_s[...] * SCALE).T
    for j in range(GROUP):
        dq_ref[0, :, j * HEAD:(j + 1) * HEAD] = dq[j * BLOCK:(j + 1) * BLOCK, :]


def write_slots(index, late, dk_s, dv_s, out_s, own_ref, other_ref):
    z, c = (index // 2) % 4, index % 2
    for kind, acc in ((0, dk_s), (1, dv_s)):
        out_s[...] = (acc[...] * SCALE).T if kind == 0 else acc[...].T
        for ref, core in ((own_ref, c), (other_ref, 1 - c)):
            for k in range(4):
                for s in range(4):
                    n = s * 8 + ((z + k) % 4) * 2 + core
                    row = (31 - n if late else n) * BLOCK
                    rows = pl.ds(pl.multiple_of(row, BLOCK), BLOCK)
                    ref[k, s, kind] = out_s[rows, :]


def own_kernel(
    index_ref, x_ref, kv_own, kv_other, dq_ref, kt_ref, vt_ref, dk_ref, dv_ref,
    *scratch,
):
    k_s, v_s, dq_s, rel_s, *work = scratch
    half = pl.program_id(0)
    index = index_ref[0]
    y, z, c = index // 8, (index // 2) % 4, index % 2
    owner = owner_of(index, 0)
    block = jnp.where(half == 0, owner, 63 - owner)

    @pl.when(half == 0)
    def _():
        relative(rel_s)
        dk_ref[...] = jnp.zeros_like(dk_ref)
        dv_ref[...] = jnp.zeros_like(dv_ref)
        for ref, core in ((kv_own, c), (kv_other, 1 - c)):
            for k in range(4):
                for s in range(4):
                    n = ((y + 4 - STEPS[s]) % 4) * 8 + ((z - k + 4) % 4) * 2 + core
                    for a in range(2):
                        row = (n if a == 0 else 63 - n) * BLOCK
                        rows = pl.ds(pl.multiple_of(row, BLOCK), BLOCK)
                        k_s[rows, :] = ref[k, s, 0, a]
                        v_s[rows, :] = ref[k, s, 1, a]
        kt_ref[...] = k_s[...].T
        vt_ref[...] = v_s[...].T

    load_block(x_ref, work)
    dq_s[...] = jnp.zeros_like(dq_s)
    full = block // (TILE // BLOCK)
    sweep(block, 0, full, True, 0, kt_ref, vt_ref, dk_ref, dv_ref, dq_s, work, rel_s)
    write_queries(dq_s, dq_ref)


def late_kernel(
    index_ref, x1, x2, x3, kt_ref, vt_ref, dk_in, dv_in, dq_ref, own_ref, other_ref,
    *scratch,
):
    dk_s, dv_s, out_s, dq_s, rel_s, *work = scratch
    step = pl.program_id(0)
    index = index_ref[0]

    @pl.when(step == 0)
    def _():
        relative(rel_s)
        dk_s[...] = dk_in[...]
        dv_s[...] = dv_in[...]

    for p, x_ref in enumerate((x1, x2, x3)):
        pl.when(step == p)(lambda x_ref=x_ref: load_block(x_ref, work))
    back = jnp.where(step == 0, STEPS[1], jnp.where(step == 1, STEPS[2], STEPS[3]))
    block = 63 - owner_of(index, back)
    dq_s[...] = jnp.zeros_like(dq_s)
    full = block // (TILE // BLOCK)
    sweep(
        block, HALF // TILE, full, True, HALF, kt_ref, vt_ref, dk_s, dv_s, dq_s, work,
        rel_s,
    )
    dq_ref[0] = dq_s[...]

    @pl.when(step == 2)
    def _():
        write_slots(index, True, dk_s, dv_s, out_s, own_ref, other_ref)


def early_kernel(pairs, last, index_ref, *refs):
    count = len(pairs)
    x_refs, refs = refs[:count], refs[count:]
    kt_ref, vt_ref, dk_in, dv_in, dq_in, dq_ref, *rest = refs
    if last:
        own_ref, other_ref, dk_s, dv_s, out_s, dq_s, rel_s, *work = rest
    else:
        dk_s, dv_s, dq_s, rel_s, *work = rest
    step = pl.program_id(0)
    index = index_ref[0]
    back = STEPS[pairs[0]]
    if count == 2:
        back = jnp.where(step < 2, back, STEPS[pairs[1]])
    owner = owner_of(index, back)
    first = step % 2 == 0
    block = jnp.where(first, 63 - owner, owner)

    @pl.when(step == 0)
    def _():
        relative(rel_s)
        dk_s[...] = dk_in[...]
        dv_s[...] = dv_in[...]

    @pl.when(first)
    def _():
        dq_s[...] = dq_in[0]

    @pl.when(step % 2 == 1)
    def _():
        dq_s[...] = jnp.zeros_like(dq_s)

    if count == 1:
        load_block(x_refs[0], work)
    else:
        for p, x_ref in enumerate(x_refs):
            pl.when(step // 2 == p)(lambda x_ref=x_ref: load_block(x_ref, work))
    full = jnp.minimum(block // (TILE // BLOCK), HALF // TILE)
    sweep(
        block, 0, full, step % 2 == 1, 0, kt_ref, vt_ref, dk_s, dv_s, dq_s, work, rel_s
    )
    write_queries(dq_s, dq_ref)

    if last:
        @pl.when(step == 2 * count - 1)
        def _():
            write_slots(index, False, dk_s, dv_s, out_s, own_ref, other_ref)


WORK = [
    pltpu.VMEM((HEAD, ROWS), F32),
    pltpu.VMEM((ROWS, TILE), jnp.int32),
    pltpu.VMEM((ROWS, HEAD), BF16),
    pltpu.VMEM((ROWS, HEAD), BF16),
    pltpu.VMEM((HEAD, 2 * ROWS), BF16),
    pltpu.VMEM((HEAD, 2 * ROWS), BF16),
    pltpu.VMEM((ROWS, HEAD), F32),
    pltpu.VMEM((ROWS, HEAD), F32),
]
PACKED = 2 * WIDTH + HEAD
X_BLOCK = (1, BLOCK, PACKED)
SLOTS = (4, 4, 2, BLOCK, HEAD)


def whole(shape):
    return pl.BlockSpec(shape, lambda i, p: (0,) * len(shape))


def half_of(which):
    return pl.BlockSpec((HEAD, HALF), lambda i, p: (0, which))


def call(kernel, steps, ins, outs, scratch, micros):
    return pl.pallas_call(
        kernel,
        grid_spec=pltpu.PrefetchScalarGridSpec(
            num_scalar_prefetch=1,
            grid=(steps,),
            in_specs=ins,
            out_specs=[spec for spec, _ in outs],
            scratch_shapes=scratch,
        ),
        out_shape=[shape for _, shape in outs],
        compiler_params=pltpu.CompilerParams(
            dimension_semantics=("arbitrary",), vmem_limit_bytes=VMEM_LIMIT
        ),
        cost_estimate=pl.CostEstimate(
            flops=int(micros * 5e8), transcendentals=0, bytes_accessed=8 * 2**20
        ),
    )


DQ_BLOCK = (1, BLOCK, WIDTH)


def own_call(index, x, kv_own, kv_other):
    keys = 2 * HALF
    kv_shape = (4, 4, 2, 2, BLOCK, HEAD)
    return call(
        own_kernel,
        2,
        [pl.BlockSpec(X_BLOCK, lambda i, p: (i, 0, 0)), whole(kv_shape), whole(kv_shape)],
        [
            (
                pl.BlockSpec(DQ_BLOCK, lambda i, p: (i, 0, 0)),
                jax.ShapeDtypeStruct((2, BLOCK, WIDTH), F32),
            ),
            (whole((HEAD, keys)), jax.ShapeDtypeStruct((HEAD, keys), BF16)),
            (whole((HEAD, keys)), jax.ShapeDtypeStruct((HEAD, keys), BF16)),
            (whole((HEAD, keys)), jax.ShapeDtypeStruct((HEAD, keys), F32)),
            (whole((HEAD, keys)), jax.ShapeDtypeStruct((HEAD, keys), F32)),
        ],
        [pltpu.VMEM((keys, HEAD), BF16)] * 2 + WORK,
        13,
    )(index, x, kv_own, kv_other)


SLOT_OUTS = [(whole(SLOTS), jax.ShapeDtypeStruct(SLOTS, F32))] * 2
ACCUMULATORS = [pltpu.VMEM((HEAD, HALF), F32)] * 2
TURNED = [pltpu.VMEM((HALF, HEAD), F32)]


def late_call(index, xs, kt, vt, dk, dv):
    return call(
        late_kernel,
        3,
        [pl.BlockSpec(X_BLOCK, lambda i, p: (1, 0, 0))] * 3 + [half_of(1)] * 4,
        [
            (
                pl.BlockSpec((1, HEAD, ROWS), lambda i, p: (i, 0, 0)),
                jax.ShapeDtypeStruct((3, HEAD, ROWS), F32),
            )
        ] + SLOT_OUTS,
        ACCUMULATORS + TURNED + WORK,
        10,
    )(index, *xs, kt, vt, dk, dv)


def early_call(pairs, index, xs, kt, vt, dk, dv, dq):
    count, last = len(pairs), pairs[-1] == 3
    acc = [(whole((HEAD, HALF)), jax.ShapeDtypeStruct((HEAD, HALF), F32))] * 2
    return call(
        lambda *refs: early_kernel(pairs, last, *refs),
        2 * count,
        [pl.BlockSpec(X_BLOCK, lambda i, p: (1 - i % 2, 0, 0))] * count
        + [half_of(0)] * 4
        + [pl.BlockSpec((1, HEAD, ROWS), lambda i, p: (pairs[0] - 1 + i // 2, 0, 0))],
        [
            (
                pl.BlockSpec(DQ_BLOCK, lambda i, p: ((i // 2) * 2 + 1 - i % 2, 0, 0)),
                jax.ShapeDtypeStruct((2 * count, BLOCK, WIDTH), F32),
            )
        ] + (SLOT_OUTS if last else acc),
        (ACCUMULATORS + TURNED if last else []) + WORK,
        9 * count,
    )(index, *[xs[p] for p in pairs], kt, vt, dk, dv, dq)


def kv_pack_kernel(index_ref, k_ref, v_ref, *outs):
    y = index_ref[0] // 8
    for p, out in enumerate(outs):
        at = pl.multiple_of(((y + STEPS[p]) % 4) * HEAD, HEAD)
        out[0] = k_ref[0, :, :, pl.ds(at, HEAD)]
        out[1] = v_ref[0, :, :, pl.ds(at, HEAD)]


def kv_pack(index, keys, values):
    shape = (2, 2, BLOCK, HEAD)
    return call(
        kv_pack_kernel,
        1,
        [whole(keys.shape)] * 2,
        [(whole(shape), jax.ShapeDtypeStruct(shape, BF16))] * 4,
        [],
        1,
    )(index, keys, values)


def x_pack_kernel(index_ref, q_ref, d_ref, o_ref, log_ref, *outs):
    y = index_ref[0] // 8
    for p, out in enumerate(outs):
        head = (y + STEPS[p]) % 4
        at = pl.multiple_of(head * WIDTH, WIDTH)
        for a in range(2):
            q = q_ref[0, a, :, pl.ds(at, WIDTH)]
            d = d_ref[0, a, :, pl.ds(at, WIDTH)]
            o = o_ref[0, a, :, pl.ds(at, WIDTH)]
            out[a, :, 0:WIDTH] = q
            out[a, :, WIDTH:2 * WIDTH] = d
            product = d.astype(F32) * o.astype(F32)
            logs = log_ref[0, a]
            mine = logs[:, 0:GROUP]
            for h in range(1, HEADS):
                mine = jnp.where(head == h, logs[:, h * GROUP:(h + 1) * GROUP], mine)
            rows = jnp.concatenate(
                [mine]
                + [
                    jnp.sum(product[:, j * HEAD:(j + 1) * HEAD], 1, keepdims=True)
                    for j in range(GROUP)
                ],
                1,
            )
            high = rows.astype(BF16).astype(F32)
            middle = (rows - high).astype(BF16).astype(F32)
            low = rows - high - middle
            nothing = jnp.zeros((BLOCK, HEAD - 48), F32)
            out[a, :, 2 * WIDTH:] = jnp.concatenate(
                [high, middle, low, nothing], 1
            ).astype(BF16)


def x_pack(index, queries, output_grad, output, logs):
    shape = (2, BLOCK, PACKED)
    return call(
        x_pack_kernel,
        1,
        [whole(a.shape) for a in (queries, output_grad, output, logs)],
        [(whole(shape), jax.ShapeDtypeStruct(shape, BF16))] * 4,
        [],
        3,
    )(index, queries, output_grad, output, logs)


def finish_kernel(index_ref, both_ref, k_ref, v_ref):
    for h in range(HEADS):
        for a in range(2):
            cols = slice(h * HEAD, (h + 1) * HEAD)
            k_ref[0, a, :, cols] = both_ref[h, a, 0]
            v_ref[0, a, :, cols] = both_ref[h, a, 1]


def finish(index, both):
    shape = (1, 2, BLOCK, HEADS * HEAD)
    return call(
        finish_kernel,
        1,
        [whole(both.shape)],
        [(whole(shape), jax.ShapeDtypeStruct(shape, F32))] * 2,
        [],
        1,
    )(index, both)


def place_kernel(index_ref, *refs):
    *ins, out = refs
    y = index_ref[0] // 8
    for p, ref in enumerate(ins):
        at = ((y + STEPS[p]) % 4) * WIDTH
        out[:, :, pl.ds(pl.multiple_of(at, WIDTH), WIDTH)] = ref[...]


def place_queries(index, backs):
    shape = (2, BLOCK, HEADS * WIDTH)
    return call(
        place_kernel,
        1,
        [whole((2, BLOCK, WIDTH))] * 4,
        [(whole(shape), jax.ShapeDtypeStruct(shape, F32))],
        [],
        2,
    )(index, *backs)[0]


def body(queries, keys, values, output, output_grad, logs):
    index = lax.axis_index("seq").astype(jnp.int32)
    send = lambda a, perm: lax.ppermute(a, "seq", perm)

    place = index.reshape(1)
    pieces = list(kv_pack(place, keys, values))
    for p in (1, 2, 3):
        pieces[p] = send(pieces[p], along_y(STEPS[p]))
    kv = jnp.stack(pieces)

    xs = list(x_pack(place, queries, output_grad, output, logs))
    for p in (1, 2, 3):
        xs[p] = send(xs[p], along_y(STEPS[p]))
    slots = [kv]
    for k in (1, 2, 3):
        slots.append(send(kv, along_z(k)))
    kv_own = jnp.stack(slots)
    kv_other = send(kv_own, OTHER_CORE)

    def summed(own, other):
        other = send(other, OTHER_CORE)
        mine = own[0] + other[0]
        for k in (1, 2, 3):
            part = own[k] + other[k]
            part = send(part, along_z(k))
            mine = mine + part
        return mine

    def to_owners(mine):
        return lax.all_to_all(
            mine, "seq", 0, 0, axis_index_groups=Y_GROUPS, tiled=True
        )

    dq_own, kt, vt, dk, dv = own_call(place, xs[0], kv_own, kv_other)
    dq_late, own, other = late_call(place, xs[1:], kt, vt, dk, dv)
    late = summed(own, other)
    dq_12, dk, dv = early_call((1, 2), place, xs, kt, vt, dk, dv, dq_late)
    dq_3, own, other = early_call((3,), place, xs, kt, vt, dk, dv, dq_late)
    early = summed(own, other)
    both = to_owners(jnp.stack([early, late], 1))
    key_gradient, value_gradient = finish(place, both)
    dq = [dq_own, dq_12[0:2], dq_12[2:4], dq_3]

    backs = [dq[0]]
    for p in (1, 2, 3):
        backs.append(send(dq[p], along_y(-STEPS[p])))
    grad_query = place_queries(place, backs)

    return grad_query[None], key_gradient, value_gradient


def solution(mesh):
    placed = P("seq", None, "dp", None)

    return jax.shard_map(
        body,
        mesh=mesh,
        in_specs=(placed,) * 6,
        out_specs=(placed,) * 3,
        check_vma=False,
    )
```

profile of v0, /device:TPU:0, one launch (start us, length us, event | category | flops | bytes accessed | tf_op | source)
XLA Modules:
  0.0 141.5 jit_solution(14202697462461260204)
XLA Ops:
  2.5 1.8 %collective-permute-start = (bf16[2,2,64,128]{3,2,1,0:T(8,128)(2,1)S(1)}, bf16[2,2,64,128]{3,2,1,0:T(8,128)(2,1)S(1)}, u32[]{:S(2)}, u32[]{:S(2)}) collective-permute-start(bf16[2,2,64,128]{3,2,1,0:T(8,128)(2,1)S(1)} %get-tuple-element.29), channel_id=1, source_target_pairs={{0,32},{4,36},{8,40},{12,44},{16,48},{20,52},{24,56},{28,60},{32,6... | collective-permute-start | bytes 196616 | tf_op jit(solution)/shard_map/ppermute | solution.py:462
  5.8 2.1 %collective-permute-start.2 = (bf16[2,2,64,128]{3,2,1,0:T(8,128)(2,1)S(1)}, bf16[2,2,64,128]{3,2,1,0:T(8,128)(2,1)S(1)}, u32[]{:S(2)}, u32[]{:S(2)}) collective-permute-start(bf16[2,2,64,128]{3,2,1,0:T(8,128)(2,1)S(1)} %get-tuple-element.31), channel_id=1, source_target_pairs={{0,64},{4,68},{8,72},{12,76},{16,80},{20,84},{24,88},{28,92},{32,9... | collective-permute-start | bytes 196616 | tf_op jit(solution)/shard_map/ppermute | solution.py:462
  8.6 3.0 %collective-permute-done.2 = bf16[2,2,64,128]{3,2,1,0:T(8,128)(2,1)S(1)} collective-permute-done((bf16[2,2,64,128]{3,2,1,0:T(8,128)(2,1)S(1)}, bf16[2,2,64,128]{3,2,1,0:T(8,128)(2,1)S(1)}, u32[]{:S(2)}, u32[]{:S(2)}) %collective-permute-start.2) | collective-permute-done | bytes 65568 | tf_op jit(solution)/shard_map/ppermute | solution.py:462
  11.6 4.1 %collective-permute-start.4 = (bf16[4,2,2,64,128]{4,3,2,1,0:T(8,128)(2,1)S(1)}, bf16[4,2,2,64,128]{4,3,2,1,0:T(8,128)(2,1)S(1)}, u32[]{:S(2)}, u32[]{:S(2)}) collective-permute-start(bf16[4,2,2,64,128]{4,3,2,1,0:T(8,128)(2,1)S(1)} %get-tuple-element.60), channel_id=1, source_target_pairs={{0,16},{4,20},{8,24},{12,28},{16,0},{20,4},{24,8},{28,12},{32,48},... | collective-permute-start | bytes 786440 | tf_op jit(solution)/shard_map/ppermute | solution.py:462
  16.7 2.2 %collective-permute-start.5 = (bf16[4,2,2,64,128]{4,3,2,1,0:T(8,128)(2,1)S(1)}, bf16[4,2,2,64,128]{4,3,2,1,0:T(8,128)(2,1)S(1)}, u32[]{:S(2)}, u32[]{:S(2)}) collective-permute-start(bf16[4,2,2,64,128]{4,3,2,1,0:T(8,128)(2,1)S(1)} %get-tuple-element.60), channel_id=1, source_target_pairs={{0,24},{4,28},{8,0},{12,4},{16,8},{20,12},{24,16},{28,20},{32,56},... | collective-permute-start | bytes 786440 | tf_op jit(solution)/shard_map/ppermute | solution.py:462
  18.9 3.9 %collective-permute-done.4 = bf16[4,2,2,64,128]{4,3,2,1,0:T(8,128)(2,1)S(1)} collective-permute-done((bf16[4,2,2,64,128]{4,3,2,1,0:T(8,128)(2,1)S(1)}, bf16[4,2,2,64,128]{4,3,2,1,0:T(8,128)(2,1)S(1)}, u32[]{:S(2)}, u32[]{:S(2)}) %collective-permute-start.4) | collective-permute-done | bytes 262176 | tf_op jit(solution)/shard_map/ppermute | solution.py:462
  22.9 3.2 %collective-permute-done.3 = bf16[4,2,2,64,128]{4,3,2,1,0:T(8,128)(2,1)S(1)} collective-permute-done((bf16[4,2,2,64,128]{4,3,2,1,0:T(8,128)(2,1)S(1)}, bf16[4,2,2,64,128]{4,3,2,1,0:T(8,128)(2,1)S(1)}, u32[]{:S(2)}, u32[]{:S(2)}) %collective-permute-start.3) | collective-permute-done | bytes 262176 | tf_op jit(solution)/shard_map/ppermute | solution.py:462
  28.4 2.4 %shard_map.85 = (bf16[2,64,2176]{2,1,0:T(8,128)(2,1)S(1)}, bf16[2,64,2176]{2,1,0:T(8,128)(2,1)S(1)}, bf16[2,64,2176]{2,1,0:T(8,128)(2,1)S(1)}, bf16[2,64,2176]{2,1,0:T(8,128)(2,1)S(1)}) custom-call(s32[1]{0:T(128)} %bitcast.index_ref.refs_0_, bf16[1,2,64,4096]{3,2,1,0:T(8,128)(2,1)S(1)} %copy-done, bf16[1,2,64,4096]{3,2,1,0:T(8,128)(2,1)S(1)} %copy-done.1, ...), custom_call_target="tpu_custom_call" | custom-call | flops 1500000000 | bytes 8388608 | tf_op jit(solution)/shard_map/pallas_call | solution.py:410
  31.3 2.8 %collective-permute-start.8 = (bf16[2,64,2176]{2,1,0:T(8,128)(2,1)S(1)}, bf16[2,64,2176]{2,1,0:T(8,128)(2,1)S(1)}, u32[]{:S(2)}, u32[]{:S(2)}) collective-permute-start(bf16[2,64,2176]{2,1,0:T(8,128)(2,1)S(1)} %get-tuple-element.34), channel_id=1, source_target_pairs={{0,96},{4,100},{8,104},{12,108},{16,112},{20,116},{24,120},{28,124... | collective-permute-start | bytes 1671176 | tf_op jit(solution)/shard_map/ppermute | solution.py:462
  34.7 12.5 %shard_map.87 = (f32[2,64,1024]{2,1,0:T(8,128)S(1)}, bf16[128,4096]{1,0:T(8,128)(2,1)S(1)}, bf16[128,4096]{1,0:T(8,128)(2,1)S(1)}, f32[128,4096]{1,0:T(8,128)S(1)}, f32[128,4096]{1,0:T(8,128)S(1)}) custom-call(s32[1]{0:T(128)} %bitcast.index_ref.refs_0_, bf16[2,64,2176]{2,1,0:T(8,128)(2,1)S(1)} %get-tuple-element.27.x_ref, ...), custom_call_target="tpu_custom_call" | custom-call | flops 6499999744 | bytes 8388608 | tf_op jit(solution)/shard_map/pallas_call | solution.py:295
  47.5 10.9 %collective-permute-done.8.x2.refs_2_ = bf16[2,64,2176]{2,1,0:T(8,128)(2,1)S(1)} collective-permute-done((bf16[2,64,2176]{2,1,0:T(8,128)(2,1)S(1)}, bf16[2,64,2176]{2,1,0:T(8,128)(2,1)S(1)}, u32[]{:S(2)}, u32[]{:S(2)}) %collective-permute-start.8) | collective-permute-done | bytes 557088 | tf_op jit(solution)/shard_map/ppermute | solution.py:462
  59.1 8.8 %shard_map.88 = (f32[3,128,512]{2,1,0:T(8,128)S(1)}, f32[4,4,2,64,128]{4,3,2,1,0:T(8,128)S(1)}, f32[4,4,2,64,128]{4,3,2,1,0:T(8,128)S(1)}) custom-call(s32[1]{0:T(128)} %bitcast.index_ref.refs_0_, bf16[2,64,2176]{2,1,0:T(8,128)(2,1)S(1)} %collective-permute-done.7.x1.refs_1_, bf16[2,64,2176]{2,1,0:T(8,128)(2,1)S(1)} %collective-permute-done.8.x2.refs_2_, ...), custom_call_target="tpu_custom_call" | custom-call | flops 5000000000 | bytes 8388608 | tf_op jit(solution)/shard_map/pallas_call | solution.py:320
  67.9 17.0 %shard_map.89 = (f32[4,64,1024]{2,1,0:T(8,128)S(1)}, f32[128,2048]{1,0:T(8,128)S(1)}, f32[128,2048]{1,0:T(8,128)S(1)}) custom-call(s32[1]{0:T(128)} %bitcast.index_ref.refs_0_, bf16[2,64,2176]{2,1,0:T(8,128)(2,1)S(1)} %collective-permute-done.7.x1.refs_1_, bf16[2,64,2176]{2,1,0:T(8,128)(2,1)S(1)} %collective-permute-done.8.x2.refs_2_, ...), custom_call_target="tpu_custom_call" | custom-call | flops 8999999488 | bytes 8388608 | tf_op jit(solution)/shard_map/pallas_call | solution.py:338
  85.0 9.4 %shard_map.90 = (f32[2,64,1024]{2,1,0:T(8,128)S(1)}, f32[4,4,2,64,128]{4,3,2,1,0:T(8,128)S(1)}, f32[4,4,2,64,128]{4,3,2,1,0:T(8,128)S(1)}) custom-call(s32[1]{0:T(128)} %bitcast.index_ref.refs_0_, bf16[2,64,2176]{2,1,0:T(8,128)(2,1)S(1)} %collective-permute-done.9.x3.refs_1_, bf16[128,4096]{1,0:T(8,128)(2,1)S(1)} %get-tuple-element.35.kt_ref.refs_3_.refs_2_, ...), custom_call_target="tpu_custom_call" | custom-call | flops 4499999744 | bytes 8388608 | tf_op jit(solution)/shard_map/pallas_call | solution.py:338
  95.0 2.1 %collective-permute-done.13 = f32[4,4,2,64,128]{4,3,2,1,0:T(8,128)S(1)} collective-permute-done((f32[4,4,2,64,128]{4,3,2,1,0:T(8,128)S(1)}, f32[4,4,2,64,128]{4,3,2,1,0:T(8,128)S(1)}, u32[]{:S(2)}, u32[]{:S(2)}) %collective-permute-start.13) | collective-permute-done | bytes 1048608 | tf_op jit(solution)/shard_map/ppermute | solution.py:462
  98.4 2.2 %collective-permute-start.16 = (f32[4,2,64,128]{3,2,1,0:T(8,128)S(1)}, f32[4,2,64,128]{3,2,1,0:T(8,128)S(1)}, u32[]{:S(2)}, u32[]{:S(2)}) collective-permute-start(f32[4,2,64,128]{3,2,1,0:T(8,128)S(1)} %get-tuple-element.52), channel_id=1, source_target_pairs={{0,24},{4,28},{8,0},{12,4},{16,8},{20,12},{24,16},{28,20},{32,56},... | collective-permute-start | bytes 786440 | tf_op jit(solution)/shard_map/ppermute | solution.py:462
  103.6 2.1 %collective-permute-start.10 = (f32[2,64,1024]{2,1,0:T(8,128)}, f32[2,64,1024]{2,1,0:T(8,128)S(1)}, u32[]{:S(2)}, u32[]{:S(2)}) collective-permute-start(f32[2,64,1024]{2,1,0:T(8,128)} %get-tuple-element.58), channel_id=1, source_target_pairs={{0,96},{4,100},{8,104},{12,108},{16,112},{20,116},{24,120},{28,124... | collective-permute-start | bytes 1572872 | tf_op jit(solution)/shard_map/ppermute | solution.py:462
  107.5 4.5 %collective-permute-done.16 = f32[4,2,64,128]{3,2,1,0:T(8,128)S(1)} collective-permute-done((f32[4,2,64,128]{3,2,1,0:T(8,128)S(1)}, f32[4,2,64,128]{3,2,1,0:T(8,128)S(1)}, u32[]{:S(2)}, u32[]{:S(2)}) %collective-permute-start.16) | collective-permute-done | bytes 262176 | tf_op jit(solution)/shard_map/ppermute | solution.py:462
  112.0 4.0 %collective-permute-start.20 = (f32[4,2,64,128]{3,2,1,0:T(8,128)S(1)}, f32[4,2,64,128]{3,2,1,0:T(8,128)S(1)}, u32[]{:S(2)}, u32[]{:S(2)}) collective-permute-start(f32[4,2,64,128]{3,2,1,0:T(8,128)S(1)} %get-tuple-element.55), channel_id=1, source_target_pairs={{0,24},{4,28},{8,0},{12,4},{16,8},{20,12},{24,16},{28,20},{32,56},... | collective-permute-start | bytes 786440 | tf_op jit(solution)/shard_map/ppermute | solution.py:462
  116.1 3.6 %collective-permute-done.18 = f32[4,2,64,128]{3,2,1,0:T(8,128)S(1)} collective-permute-done((f32[4,2,64,128]{3,2,1,0:T(8,128)S(1)}, f32[4,2,64,128]{3,2,1,0:T(8,128)S(1)}, u32[]{:S(2)}, u32[]{:S(2)}) %collective-permute-start.18) | collective-permute-done | bytes 262176 | tf_op jit(solution)/shard_map/ppermute | solution.py:462
  120.5 3.4 %collective-permute-done.20 = f32[4,2,64,128]{3,2,1,0:T(8,128)S(1)} collective-permute-done((f32[4,2,64,128]{3,2,1,0:T(8,128)S(1)}, f32[4,2,64,128]{3,2,1,0:T(8,128)S(1)}, u32[]{:S(2)}, u32[]{:S(2)}) %collective-permute-start.20) | collective-permute-done | bytes 262176 | tf_op jit(solution)/shard_map/ppermute | solution.py:462
  125.6 4.1 %all-to-all-start = ((f32[4,2,2,64,128]{4,3,2,1,0:T(8,128)}), f32[4,2,2,64,128]{4,3,2,1,0:T(8,128)S(1)}, u32[]{:S(2)}, u32[]{:S(2)}) async-start(f32[4,2,2,64,128]{4,3,2,1,0:T(8,128)} %pad_maximum_fusion.1), calls=%async_computation | async-start | bytes 1048576 | tf_op jit(solution)/shard_map/all_to_all | solution.py:489
  129.7 6.4 %collective-permute-done.12.refs_3_ = f32[2,64,1024]{2,1,0:T(8,128)S(1)} collective-permute-done((f32[2,64,1024]{2,1,0:T(8,128)S(1)}, f32[2,64,1024]{2,1,0:T(8,128)S(1)}, u32[]{:S(2)}, u32[]{:S(2)}) %collective-permute-start.12) | collective-permute-done | bytes 524320 | tf_op jit(solution)/shard_map/ppermute | solution.py:462
  137.6 3.1 %all-to-all-done.both_ref = f32[4,2,2,64,128]{4,3,2,1,0:T(8,128)S(1)} async-done(((f32[4,2,2,64,128]{4,3,2,1,0:T(8,128)}), f32[4,2,2,64,128]{4,3,2,1,0:T(8,128)S(1)}, u32[]{:S(2)}, u32[]{:S(2)}) %all-to-all-start) | async-done | bytes 524320 | tf_op jit(solution)/shard_map/all_to_all | solution.py:489
  (49 shorter events, 21.0 us)
Async XLA Ops:
  2.4 24.7 %copy-start = (bf16[1,2,64,4096]{3,2,1,0:T(8,128)(2,1)S(1)}, bf16[1,2,64,4096]{3,2,1,0:T(8,128)(2,1)}, u32[]{:S(2)}) copy-start(bf16[1,2,64,4096]{3,2,1,0:T(8,128)(2,1)} %q_ref.1) | copy-start | bytes 3145732
  2.5 24.7 %copy-start.1 = (bf16[1,2,64,4096]{3,2,1,0:T(8,128)(2,1)S(1)}, bf16[1,2,64,4096]{3,2,1,0:T(8,128)(2,1)}, u32[]{:S(2)}) copy-start(bf16[1,2,64,4096]{3,2,1,0:T(8,128)(2,1)} %d_ref.1) | copy-start | bytes 3145732
  2.5 5.5 %collective-permute-start = (bf16[2,2,64,128]{3,2,1,0:T(8,128)(2,1)S(1)}, bf16[2,2,64,128]{3,2,1,0:T(8,128)(2,1)S(1)}, u32[]{:S(2)}, u32[]{:S(2)}) collective-permute-start(bf16[2,2,64,128]{3,2,1,0:T(8,128)(2,1)S(1)} %get-tuple-element.29), channel_id=1, source_target_pairs={{0,32},{4,36},{8,40},{12,44},{16,48},{20,52},{24,56},{28,60},{32,6... | collective-permute-start | bytes 196616 | tf_op jit(solution)/shard_map/ppermute | solution.py:462
  4.3 4.4 %collective-permute-start.1 = (bf16[2,2,64,128]{3,2,1,0:T(8,128)(2,1)S(1)}, bf16[2,2,64,128]{3,2,1,0:T(8,128)(2,1)S(1)}, u32[]{:S(2)}, u32[]{:S(2)}) collective-permute-start(bf16[2,2,64,128]{3,2,1,0:T(8,128)(2,1)S(1)} %get-tuple-element.30), channel_id=1, source_target_pairs={{0,96},{4,100},{8,104},{12,108},{16,112},{20,116},{24,120},{28,124... | collective-permute-start | bytes 196616 | tf_op jit(solution)/shard_map/ppermute | solution.py:462
  5.8 5.8 %collective-permute-start.2 = (bf16[2,2,64,128]{3,2,1,0:T(8,128)(2,1)S(1)}, bf16[2,2,64,128]{3,2,1,0:T(8,128)(2,1)S(1)}, u32[]{:S(2)}, u32[]{:S(2)}) collective-permute-start(bf16[2,2,64,128]{3,2,1,0:T(8,128)(2,1)S(1)} %get-tuple-element.31), channel_id=1, source_target_pairs={{0,64},{4,68},{8,72},{12,76},{16,80},{20,84},{24,88},{28,92},{32,9... | collective-permute-start | bytes 196616 | tf_op jit(solution)/shard_map/ppermute | solution.py:462
  11.6 11.2 %collective-permute-start.4 = (bf16[4,2,2,64,128]{4,3,2,1,0:T(8,128)(2,1)S(1)}, bf16[4,2,2,64,128]{4,3,2,1,0:T(8,128)(2,1)S(1)}, u32[]{:S(2)}, u32[]{:S(2)}) collective-permute-start(bf16[4,2,2,64,128]{4,3,2,1,0:T(8,128)(2,1)S(1)} %get-tuple-element.60), channel_id=1, source_target_pairs={{0,16},{4,20},{8,24},{12,28},{16,0},{20,4},{24,8},{28,12},{32,48},... | collective-permute-start | bytes 786440 | tf_op jit(solution)/shard_map/ppermute | solution.py:462
  15.7 10.4 %collective-permute-start.3 = (bf16[4,2,2,64,128]{4,3,2,1,0:T(8,128)(2,1)S(1)}, bf16[4,2,2,64,128]{4,3,2,1,0:T(8,128)(2,1)S(1)}, u32[]{:S(2)}, u32[]{:S(2)}) collective-permute-start(bf16[4,2,2,64,128]{4,3,2,1,0:T(8,128)(2,1)S(1)} %get-tuple-element.60), channel_id=1, source_target_pairs={{0,8},{4,12},{8,16},{12,20},{16,24},{20,28},{24,0},{28,4},{32,40},... | collective-permute-start | bytes 786440 | tf_op jit(solution)/shard_map/ppermute | solution.py:462
  16.7 10.1 %collective-permute-start.5 = (bf16[4,2,2,64,128]{4,3,2,1,0:T(8,128)(2,1)S(1)}, bf16[4,2,2,64,128]{4,3,2,1,0:T(8,128)(2,1)S(1)}, u32[]{:S(2)}, u32[]{:S(2)}) collective-permute-start(bf16[4,2,2,64,128]{4,3,2,1,0:T(8,128)(2,1)S(1)} %get-tuple-element.60), channel_id=1, source_target_pairs={{0,24},{4,28},{8,0},{12,4},{16,8},{20,12},{24,16},{28,20},{32,56},... | collective-permute-start | bytes 786440 | tf_op jit(solution)/shard_map/ppermute | solution.py:462
  26.9 7.8 %collective-permute-start.6 = (bf16[4,4,2,2,64,128]{5,4,3,2,1,0:T(8,128)(2,1)S(1)}, bf16[4,4,2,2,64,128]{5,4,3,2,1,0:T(8,128)(2,1)}, u32[]{:S(2)}, u32[]{:S(2)}) collective-permute-start(bf16[4,4,2,2,64,128]{5,4,3,2,1,0:T(8,128)(2,1)S(1)} %pad_maximum_fusion.kv_own), channel_id=1, source_target_pairs={{0,4},{4,0},{8,12},{12,8},{16,20},{20,16},{24,28},{28,24},{32,36},... | collective-permute-start | bytes 3145736 | tf_op jit(solution)/shard_map/ppermute | solution.py:462
  30.8 16.7 %collective-permute-start.7 = (bf16[2,64,2176]{2,1,0:T(8,128)(2,1)S(1)}, bf16[2,64,2176]{2,1,0:T(8,128)(2,1)S(1)}, u32[]{:S(2)}, u32[]{:S(2)}) collective-permute-start(bf16[2,64,2176]{2,1,0:T(8,128)(2,1)S(1)} %get-tuple-element.33), channel_id=1, source_target_pairs={{0,32},{4,36},{8,40},{12,44},{16,48},{20,52},{24,56},{28,60},{32,6... | collective-permute-start | bytes 1671176 | tf_op jit(solution)/shard_map/ppermute | solution.py:462
  31.3 27.0 %collective-permute-start.8 = (bf16[2,64,2176]{2,1,0:T(8,128)(2,1)S(1)}, bf16[2,64,2176]{2,1,0:T(8,128)(2,1)S(1)}, u32[]{:S(2)}, u32[]{:S(2)}) collective-permute-start(bf16[2,64,2176]{2,1,0:T(8,128)(2,1)S(1)} %get-tuple-element.34), channel_id=1, source_target_pairs={{0,96},{4,100},{8,104},{12,108},{16,112},{20,116},{24,120},{28,124... | collective-permute-start | bytes 1671176 | tf_op jit(solution)/shard_map/ppermute | solution.py:462
  34.1 25.0 %collective-permute-start.9 = (bf16[2,64,2176]{2,1,0:T(8,128)(2,1)S(1)}, bf16[2,64,2176]{2,1,0:T(8,128)(2,1)S(1)}, u32[]{:S(2)}, u32[]{:S(2)}) collective-permute-start(bf16[2,64,2176]{2,1,0:T(8,128)(2,1)S(1)} %get-tuple-element.39), channel_id=1, source_target_pairs={{0,64},{4,68},{8,72},{12,76},{16,80},{20,84},{24,88},{28,92},{32,9... | collective-permute-start | bytes 1671176 | tf_op jit(solution)/shard_map/ppermute | solution.py:462
  94.4 2.7 %collective-permute-start.13 = (f32[4,4,2,64,128]{4,3,2,1,0:T(8,128)S(1)}, f32[4,4,2,64,128]{4,3,2,1,0:T(8,128)S(1)}, u32[]{:S(2)}, u32[]{:S(2)}) collective-permute-start(f32[4,4,2,64,128]{4,3,2,1,0:T(8,128)S(1)} %get-tuple-element.46), channel_id=1, source_target_pairs={{0,4},{4,0},{8,12},{12,8},{16,20},{20,16},{24,28},{28,24},{32,36},... | collective-permute-start | bytes 3145736 | tf_op jit(solution)/shard_map/ppermute | solution.py:462
  94.5 9.1 %collective-permute-start.17 = (f32[4,4,2,64,128]{4,3,2,1,0:T(8,128)S(1)}, f32[4,4,2,64,128]{4,3,2,1,0:T(8,128)S(1)}, u32[]{:S(2)}, u32[]{:S(2)}) collective-permute-start(f32[4,4,2,64,128]{4,3,2,1,0:T(8,128)S(1)} %get-tuple-element.48), channel_id=1, source_target_pairs={{0,4},{4,0},{8,12},{12,8},{16,20},{20,16},{24,28},{28,24},{32,36},... | collective-permute-start | bytes 3145736 | tf_op jit(solution)/shard_map/ppermute | solution.py:462
  97.2 9.6 %collective-permute-start.14 = (f32[4,2,64,128]{3,2,1,0:T(8,128)S(1)}, f32[4,2,64,128]{3,2,1,0:T(8,128)S(1)}, u32[]{:S(2)}, u32[]{:S(2)}) collective-permute-start(f32[4,2,64,128]{3,2,1,0:T(8,128)S(1)} %get-tuple-element.51), channel_id=1, source_target_pairs={{0,8},{4,12},{8,16},{12,20},{16,24},{20,28},{24,0},{28,4},{32,40},... | collective-permute-start | bytes 786440 | tf_op jit(solution)/shard_map/ppermute | solution.py:462
  98.4 13.7 %collective-permute-start.16 = (f32[4,2,64,128]{3,2,1,0:T(8,128)S(1)}, f32[4,2,64,128]{3,2,1,0:T(8,128)S(1)}, u32[]{:S(2)}, u32[]{:S(2)}) collective-permute-start(f32[4,2,64,128]{3,2,1,0:T(8,128)S(1)} %get-tuple-element.52), channel_id=1, source_target_pairs={{0,24},{4,28},{8,0},{12,4},{16,8},{20,12},{24,16},{28,20},{32,56},... | collective-permute-start | bytes 786440 | tf_op jit(solution)/shard_map/ppermute | solution.py:462
  100.5 15.5 %collective-permute-start.15 = (f32[4,2,64,128]{3,2,1,0:T(8,128)S(1)}, f32[4,2,64,128]{3,2,1,0:T(8,128)S(1)}, u32[]{:S(2)}, u32[]{:S(2)}) collective-permute-start(f32[4,2,64,128]{3,2,1,0:T(8,128)S(1)} %get-tuple-element.53), channel_id=1, source_target_pairs={{0,16},{4,20},{8,24},{12,28},{16,0},{20,4},{24,8},{28,12},{32,48},... | collective-permute-start | bytes 786440 | tf_op jit(solution)/shard_map/ppermute | solution.py:462
  102.5 27.2 %collective-permute-start.11 = (f32[2,64,1024]{2,1,0:T(8,128)}, f32[2,64,1024]{2,1,0:T(8,128)S(1)}, u32[]{:S(2)}, u32[]{:S(2)}) collective-permute-start(f32[2,64,1024]{2,1,0:T(8,128)} %get-tuple-element.57), channel_id=1, source_target_pairs={{0,32},{4,36},{8,40},{12,44},{16,48},{20,52},{24,56},{28,60},{32,6... | collective-permute-start | bytes 1572872 | tf_op jit(solution)/shard_map/ppermute | solution.py:462
  103.6 26.1 %collective-permute-start.10 = (f32[2,64,1024]{2,1,0:T(8,128)}, f32[2,64,1024]{2,1,0:T(8,128)S(1)}, u32[]{:S(2)}, u32[]{:S(2)}) collective-permute-start(f32[2,64,1024]{2,1,0:T(8,128)} %get-tuple-element.58), channel_id=1, source_target_pairs={{0,96},{4,100},{8,104},{12,108},{16,112},{20,116},{24,120},{28,124... | collective-permute-start | bytes 1572872 | tf_op jit(solution)/shard_map/ppermute | solution.py:462
  106.9 12.9 %collective-permute-start.18 = (f32[4,2,64,128]{3,2,1,0:T(8,128)S(1)}, f32[4,2,64,128]{3,2,1,0:T(8,128)S(1)}, u32[]{:S(2)}, u32[]{:S(2)}) collective-permute-start(f32[4,2,64,128]{3,2,1,0:T(8,128)S(1)} %get-tuple-element.54), channel_id=1, source_target_pairs={{0,8},{4,12},{8,16},{12,20},{16,24},{20,28},{24,0},{28,4},{32,40},... | collective-permute-start | bytes 786440 | tf_op jit(solution)/shard_map/ppermute | solution.py:462
  112.0 11.8 %collective-permute-start.20 = (f32[4,2,64,128]{3,2,1,0:T(8,128)S(1)}, f32[4,2,64,128]{3,2,1,0:T(8,128)S(1)}, u32[]{:S(2)}, u32[]{:S(2)}) collective-permute-start(f32[4,2,64,128]{3,2,1,0:T(8,128)S(1)} %get-tuple-element.55), channel_id=1, source_target_pairs={{0,24},{4,28},{8,0},{12,4},{16,8},{20,12},{24,16},{28,20},{32,56},... | collective-permute-start | bytes 786440 | tf_op jit(solution)/shard_map/ppermute | solution.py:462
  116.1 8.6 %collective-permute-start.19 = (f32[4,2,64,128]{3,2,1,0:T(8,128)S(1)}, f32[4,2,64,128]{3,2,1,0:T(8,128)S(1)}, u32[]{:S(2)}, u32[]{:S(2)}) collective-permute-start(f32[4,2,64,128]{3,2,1,0:T(8,128)S(1)} %get-tuple-element.56), channel_id=1, source_target_pairs={{0,16},{4,20},{8,24},{12,28},{16,0},{20,4},{24,8},{28,12},{32,48},... | collective-permute-start | bytes 786440 | tf_op jit(solution)/shard_map/ppermute | solution.py:462
  119.8 16.3 %collective-permute-start.12 = (f32[2,64,1024]{2,1,0:T(8,128)S(1)}, f32[2,64,1024]{2,1,0:T(8,128)S(1)}, u32[]{:S(2)}, u32[]{:S(2)}) collective-permute-start(f32[2,64,1024]{2,1,0:T(8,128)S(1)} %get-tuple-element.44), channel_id=1, source_target_pairs={{0,64},{4,68},{8,72},{12,76},{16,80},{20,84},{24,88},{28,92},{32,9... | collective-permute-start | bytes 1572872 | tf_op jit(solution)/shard_map/ppermute | solution.py:462
  125.6 15.1 %all-to-all-start = ((f32[4,2,2,64,128]{4,3,2,1,0:T(8,128)}), f32[4,2,2,64,128]{4,3,2,1,0:T(8,128)S(1)}, u32[]{:S(2)}, u32[]{:S(2)}) async-start(f32[4,2,2,64,128]{4,3,2,1,0:T(8,128)} %pad_maximum_fusion.1), calls=%async_computation | async-start | bytes 1048576 | tf_op jit(solution)/shard_map/all_to_all | solution.py:489
  (4 other events, 27.6 us)
where the time goes:
time: 142 us
  Pallas kernels  52.6 us (37%)
  waiting for transfers between devices  48.4 us (34%)
  starting transfers between devices  34.2 us (24%)
  local copies, waits for them, and re-layouts  4.19 us (3%)
    ppermute x21, waiting for transfers between devices, body(): send = lambda a, perm: lax.ppermute(a, 'seq', perm)  45.3 us
    ppermute x21, starting transfers between devices, body(): send = lambda a, perm: lax.ppermute(a, 'seq', perm)  30.1 us
    pallas_call x2, Pallas kernels, early_call(): call(lambda *refs: early_kernel(pairs, last, *refs), 2 * count, [pl.Block...  26.4 us
    pallas_call x1, Pallas kernels, own_call(): call(own_kernel, 2, [pl.BlockSpec(X_BLOCK, lambda i, p: (i, 0, 0)), whole...  12.5 us
    pallas_call x1, Pallas kernels, late_call(): call(late_kernel, 3, [pl.BlockSpec(X_BLOCK, lambda i, p: (1, 0, 0))] * 3...  8.81 us
    all_to_all x1, starting transfers between devices, to_owners(): lax.all_to_all(mine, 'seq', 0, 0, axis_index_groups=Y_GROUPS, tiled=True)  4.12 us
    unnamed x13, local copies, waits for them, and re-layouts  3.11 us
    all_to_all x1, waiting for transfers between devices, to_owners(): lax.all_to_all(mine, 'seq', 0, 0, axis_index_groups=Y_GROUPS, tiled=True)  3.1 us
  transfers between devices with their start and end apart: 22, of which 17 were waited for; matrix products, arithmetic and copies ran while one was open for 2% of the time, Pallas kernels for 12%

commit v1 on v0

--- a/solution.py
+++ b/solution.py
@@ -372,9 +372,9 @@
     )(index, keys, values)
 
 
-def x_pack_kernel(index_ref, q_ref, d_ref, o_ref, log_ref, *outs):
+def x_pack_kernel(slots, index_ref, q_ref, d_ref, o_ref, log_ref, *outs):
     y = index_ref[0] // 8
-    for p, out in enumerate(outs):
+    for p, out in zip(slots, outs):
         head = (y + STEPS[p]) % 4
         at = pl.multiple_of(head * WIDTH, WIDTH)
         for a in range(2):
@@ -405,13 +405,13 @@
             ).astype(BF16)
 
 
-def x_pack(index, queries, output_grad, output, logs):
+def x_pack(slots, index, queries, output_grad, output, logs):
     shape = (2, BLOCK, PACKED)
     return call(
-        x_pack_kernel,
+        lambda *refs: x_pack_kernel(slots, *refs),
         1,
         [whole(a.shape) for a in (queries, output_grad, output, logs)],
-        [(whole(shape), jax.ShapeDtypeStruct(shape, BF16))] * 4,
+        [(whole(shape), jax.ShapeDtypeStruct(shape, BF16))] * len(slots),
         [],
         3,
     )(index, queries, output_grad, output, logs)
@@ -467,7 +467,9 @@
         pieces[p] = send(pieces[p], along_y(STEPS[p]))
     kv = jnp.stack(pieces)
 
-    xs = list(x_pack(place, queries, output_grad, output, logs))
+    rows = (queries, output_grad, output, logs)
+    sent = x_pack((1, 2, 3), place, *rows)
+    xs = [*x_pack((0,), place, *rows), *sent]
     for p in (1, 2, 3):
         xs[p] = send(xs[p], along_y(STEPS[p]))
     slots = [kv]

time: 142 us -> 141 us (level)
  transfers between devices with their start and end apart: 22 -> 22, of which waited for: 17 -> 16; matrix products, arithmetic and copies ran while one was open for 2% -> 2% of each run, Pallas kernels for 12% -> 12%
where the time goes in v1:
time: 141 us
  Pallas kernels  52.5 us (37%)
  waiting for transfers between devices  47.8 us (34%)
  starting transfers between devices  34.2 us (24%)
  local copies, waits for them, and re-layouts  4.19 us (3%)
    ppermute x21, waiting for transfers between devices, body(): send = lambda a, perm: lax.ppermute(a, 'seq', perm)  44.7 us
    ppermute x21, starting transfers between devices, body(): send = lambda a, perm: lax.ppermute(a, 'seq', perm)  30.1 us
    pallas_call x2, Pallas kernels, early_call(): call(lambda *refs: early_kernel(pairs, last, *refs), 2 * count, [pl.Block...  26.4 us
    pallas_call x1, Pallas kernels, own_call(): call(own_kernel, 2, [pl.BlockSpec(X_BLOCK, lambda i, p: (i, 0, 0)), whole...  12.6 us
    pallas_call x1, Pallas kernels, late_call(): call(late_kernel, 3, [pl.BlockSpec(X_BLOCK, lambda i, p: (1, 0, 0))] * 3...  8.81 us
    all_to_all x1, starting transfers between devices, to_owners(): lax.all_to_all(mine, 'seq', 0, 0, axis_index_groups=Y_GROUPS, tiled=True)  4.12 us
    unnamed x13, local copies, waits for them, and re-layouts  3.11 us
    all_to_all x1, waiting for transfers between devices, to_owners(): lax.all_to_all(mine, 'seq', 0, 0, axis_index_groups=Y_GROUPS, tiled=True)  3.1 us
  transfers between devices with their start and end apart: 22, of which 16 were waited for; matrix products, arithmetic and copies ran while one was open for 2% of the time, Pallas kernels for 12%

profile of v1, /device:TPU:0, one launch (start us, length us, event | category | flops | bytes accessed | tf_op | source)
XLA Modules:
  0.0 140.9 jit_solution(17518462219004810332)
XLA Ops:
  2.5 1.8 %collective-permute-start = (bf16[2,2,64,128]{3,2,1,0:T(8,128)(2,1)S(1)}, bf16[2,2,64,128]{3,2,1,0:T(8,128)(2,1)S(1)}, u32[]{:S(2)}, u32[]{:S(2)}) collective-permute-start(bf16[2,2,64,128]{3,2,1,0:T(8,128)(2,1)S(1)} %get-tuple-element.27), channel_id=1, source_target_pairs={{0,32},{4,36},{8,40},{12,44},{16,48},{20,52},{24,56},{28,60},{32,6... | collective-permute-start | bytes 196616 | tf_op jit(solution)/shard_map/ppermute | solution.py:462
  5.8 2.1 %collective-permute-start.2 = (bf16[2,2,64,128]{3,2,1,0:T(8,128)(2,1)S(1)}, bf16[2,2,64,128]{3,2,1,0:T(8,128)(2,1)S(1)}, u32[]{:S(2)}, u32[]{:S(2)}) collective-permute-start(bf16[2,2,64,128]{3,2,1,0:T(8,128)(2,1)S(1)} %get-tuple-element.29), channel_id=1, source_target_pairs={{0,64},{4,68},{8,72},{12,76},{16,80},{20,84},{24,88},{28,92},{32,9... | collective-permute-start | bytes 196616 | tf_op jit(solution)/shard_map/ppermute | solution.py:462
  8.6 3.0 %collective-permute-done.2 = bf16[2,2,64,128]{3,2,1,0:T(8,128)(2,1)S(1)} collective-permute-done((bf16[2,2,64,128]{3,2,1,0:T(8,128)(2,1)S(1)}, bf16[2,2,64,128]{3,2,1,0:T(8,128)(2,1)S(1)}, u32[]{:S(2)}, u32[]{:S(2)}) %collective-permute-start.2) | collective-permute-done | bytes 65568 | tf_op jit(solution)/shard_map/ppermute | solution.py:462
  11.6 4.1 %collective-permute-start.4 = (bf16[4,2,2,64,128]{4,3,2,1,0:T(8,128)(2,1)S(1)}, bf16[4,2,2,64,128]{4,3,2,1,0:T(8,128)(2,1)S(1)}, u32[]{:S(2)}, u32[]{:S(2)}) collective-permute-start(bf16[4,2,2,64,128]{4,3,2,1,0:T(8,128)(2,1)S(1)} %get-tuple-element.58), channel_id=1, source_target_pairs={{0,16},{4,20},{8,24},{12,28},{16,0},{20,4},{24,8},{28,12},{32,48},... | collective-permute-start | bytes 786440 | tf_op jit(solution)/shard_map/ppermute | solution.py:462
  16.7 2.2 %collective-permute-start.5 = (bf16[4,2,2,64,128]{4,3,2,1,0:T(8,128)(2,1)S(1)}, bf16[4,2,2,64,128]{4,3,2,1,0:T(8,128)(2,1)S(1)}, u32[]{:S(2)}, u32[]{:S(2)}) collective-permute-start(bf16[4,2,2,64,128]{4,3,2,1,0:T(8,128)(2,1)S(1)} %get-tuple-element.58), channel_id=1, source_target_pairs={{0,24},{4,28},{8,0},{12,4},{16,8},{20,12},{24,16},{28,20},{32,56},... | collective-permute-start | bytes 786440 | tf_op jit(solution)/shard_map/ppermute | solution.py:462
  18.9 3.9 %collective-permute-done.4 = bf16[4,2,2,64,128]{4,3,2,1,0:T(8,128)(2,1)S(1)} collective-permute-done((bf16[4,2,2,64,128]{4,3,2,1,0:T(8,128)(2,1)S(1)}, bf16[4,2,2,64,128]{4,3,2,1,0:T(8,128)(2,1)S(1)}, u32[]{:S(2)}, u32[]{:S(2)}) %collective-permute-start.4) | collective-permute-done | bytes 262176 | tf_op jit(solution)/shard_map/ppermute | solution.py:462
  22.9 3.2 %collective-permute-done.3 = bf16[4,2,2,64,128]{4,3,2,1,0:T(8,128)(2,1)S(1)} collective-permute-done((bf16[4,2,2,64,128]{4,3,2,1,0:T(8,128)(2,1)S(1)}, bf16[4,2,2,64,128]{4,3,2,1,0:T(8,128)(2,1)S(1)}, u32[]{:S(2)}, u32[]{:S(2)}) %collective-permute-start.3) | collective-permute-done | bytes 262176 | tf_op jit(solution)/shard_map/ppermute | solution.py:462
  28.4 1.8 %shard_map.88 = (bf16[2,64,2176]{2,1,0:T(8,128)(2,1)S(1)}, bf16[2,64,2176]{2,1,0:T(8,128)(2,1)S(1)}, bf16[2,64,2176]{2,1,0:T(8,128)(2,1)S(1)}) custom-call(s32[1]{0:T(128)} %bitcast.refs_0_.index_ref, bf16[1,2,64,4096]{3,2,1,0:T(8,128)(2,1)S(1)} %copy-done, bf16[1,2,64,4096]{3,2,1,0:T(8,128)(2,1)S(1)} %copy-done.1, bf16[1,2,64,4096]{3,2,1,0:T(8,128)(2,1)S(1)} %copy-done.2, ...), custom_call_target="tpu_custom_call" | custom-call | flops 1500000000 | bytes 8388608 | tf_op jit(solution)/shard_map/pallas_call | solution.py:410
  30.7 2.8 %collective-permute-start.8 = (bf16[2,64,2176]{2,1,0:T(8,128)(2,1)S(1)}, bf16[2,64,2176]{2,1,0:T(8,128)(2,1)S(1)}, u32[]{:S(2)}, u32[]{:S(2)}) collective-permute-start(bf16[2,64,2176]{2,1,0:T(8,128)(2,1)S(1)} %get-tuple-element.32), channel_id=1, source_target_pairs={{0,96},{4,100},{8,104},{12,108},{16,112},{20,116},{24,120},{28,124... | collective-permute-start | bytes 1671176 | tf_op jit(solution)/shard_map/ppermute | solution.py:462
  34.7 12.6 %shard_map.87 = (f32[2,64,1024]{2,1,0:T(8,128)S(1)}, bf16[128,4096]{1,0:T(8,128)(2,1)S(1)}, bf16[128,4096]{1,0:T(8,128)(2,1)S(1)}, f32[128,4096]{1,0:T(8,128)S(1)}, f32[128,4096]{1,0:T(8,128)S(1)}) custom-call(s32[1]{0:T(128)} %bitcast.refs_0_.index_ref, bf16[2,64,2176]{2,1,0:T(8,128)(2,1)S(1)} %shard_map.85.x_ref, ...), custom_call_target="tpu_custom_call" | custom-call | flops 6499999744 | bytes 8388608 | tf_op jit(solution)/shard_map/pallas_call | solution.py:295
  47.2 10.4 %collective-permute-done.8.x2.refs_2_ = bf16[2,64,2176]{2,1,0:T(8,128)(2,1)S(1)} collective-permute-done((bf16[2,64,2176]{2,1,0:T(8,128)(2,1)S(1)}, bf16[2,64,2176]{2,1,0:T(8,128)(2,1)S(1)}, u32[]{:S(2)}, u32[]{:S(2)}) %collective-permute-start.8) | collective-permute-done | bytes 557088 | tf_op jit(solution)/shard_map/ppermute | solution.py:462
  58.5 8.8 %shard_map.89 = (f32[3,128,512]{2,1,0:T(8,128)S(1)}, f32[4,4,2,64,128]{4,3,2,1,0:T(8,128)S(1)}, f32[4,4,2,64,128]{4,3,2,1,0:T(8,128)S(1)}) custom-call(s32[1]{0:T(128)} %bitcast.refs_0_.index_ref, bf16[2,64,2176]{2,1,0:T(8,128)(2,1)S(1)} %collective-permute-done.7.x1.refs_1_, bf16[2,64,2176]{2,1,0:T(8,128)(2,1)S(1)} %collective-permute-done.8.x2.refs_2_, ...), custom_call_target="tpu_custom_call" | custom-call | flops 5000000000 | bytes 8388608 | tf_op jit(solution)/shard_map/pallas_call | solution.py:320
  67.3 17.0 %shard_map.90 = (f32[4,64,1024]{2,1,0:T(8,128)S(1)}, f32[128,2048]{1,0:T(8,128)S(1)}, f32[128,2048]{1,0:T(8,128)S(1)}) custom-call(s32[1]{0:T(128)} %bitcast.refs_0_.index_ref, bf16[2,64,2176]{2,1,0:T(8,128)(2,1)S(1)} %collective-permute-done.7.x1.refs_1_, bf16[2,64,2176]{2,1,0:T(8,128)(2,1)S(1)} %collective-permute-done.8.x2.refs_2_, ...), custom_call_target="tpu_custom_call" | custom-call | flops 8999999488 | bytes 8388608 | tf_op jit(solution)/shard_map/pallas_call | solution.py:338
  84.3 9.4 %shard_map.91 = (f32[2,64,1024]{2,1,0:T(8,128)S(1)}, f32[4,4,2,64,128]{4,3,2,1,0:T(8,128)S(1)}, f32[4,4,2,64,128]{4,3,2,1,0:T(8,128)S(1)}) custom-call(s32[1]{0:T(128)} %bitcast.refs_0_.index_ref, bf16[2,64,2176]{2,1,0:T(8,128)(2,1)S(1)} %collective-permute-done.9.x3.refs_1_, bf16[128,4096]{1,0:T(8,128)(2,1)S(1)} %get-tuple-element.33.kt_ref.refs_3_.refs_2_, ...), custom_call_target="tpu_custom_call" | custom-call | flops 4499999744 | bytes 8388608 | tf_op jit(solution)/shard_map/pallas_call | solution.py:338
  94.3 2.1 %collective-permute-done.13 = f32[4,4,2,64,128]{4,3,2,1,0:T(8,128)S(1)} collective-permute-done((f32[4,4,2,64,128]{4,3,2,1,0:T(8,128)S(1)}, f32[4,4,2,64,128]{4,3,2,1,0:T(8,128)S(1)}, u32[]{:S(2)}, u32[]{:S(2)}) %collective-permute-start.13) | collective-permute-done | bytes 1048608 | tf_op jit(solution)/shard_map/ppermute | solution.py:462
  97.7 2.2 %collective-permute-start.16 = (f32[4,2,64,128]{3,2,1,0:T(8,128)S(1)}, f32[4,2,64,128]{3,2,1,0:T(8,128)S(1)}, u32[]{:S(2)}, u32[]{:S(2)}) collective-permute-start(f32[4,2,64,128]{3,2,1,0:T(8,128)S(1)} %get-tuple-element.50), channel_id=1, source_target_pairs={{0,24},{4,28},{8,0},{12,4},{16,8},{20,12},{24,16},{28,20},{32,56},... | collective-permute-start | bytes 786440 | tf_op jit(solution)/shard_map/ppermute | solution.py:462
  102.9 2.1 %collective-permute-start.10 = (f32[2,64,1024]{2,1,0:T(8,128)}, f32[2,64,1024]{2,1,0:T(8,128)S(1)}, u32[]{:S(2)}, u32[]{:S(2)}) collective-permute-start(f32[2,64,1024]{2,1,0:T(8,128)} %get-tuple-element.56), channel_id=1, source_target_pairs={{0,96},{4,100},{8,104},{12,108},{16,112},{20,116},{24,120},{28,124... | collective-permute-start | bytes 1572872 | tf_op jit(solution)/shard_map/ppermute | solution.py:462
  106.9 4.5 %collective-permute-done.16 = f32[4,2,64,128]{3,2,1,0:T(8,128)S(1)} collective-permute-done((f32[4,2,64,128]{3,2,1,0:T(8,128)S(1)}, f32[4,2,64,128]{3,2,1,0:T(8,128)S(1)}, u32[]{:S(2)}, u32[]{:S(2)}) %collective-permute-start.16) | collective-permute-done | bytes 262176 | tf_op jit(solution)/shard_map/ppermute | solution.py:462
  111.4 4.0 %collective-permute-start.20 = (f32[4,2,64,128]{3,2,1,0:T(8,128)S(1)}, f32[4,2,64,128]{3,2,1,0:T(8,128)S(1)}, u32[]{:S(2)}, u32[]{:S(2)}) collective-permute-start(f32[4,2,64,128]{3,2,1,0:T(8,128)S(1)} %get-tuple-element.53), channel_id=1, source_target_pairs={{0,24},{4,28},{8,0},{12,4},{16,8},{20,12},{24,16},{28,20},{32,56},... | collective-permute-start | bytes 786440 | tf_op jit(solution)/shard_map/ppermute | solution.py:462
  115.5 3.6 %collective-permute-done.18 = f32[4,2,64,128]{3,2,1,0:T(8,128)S(1)} collective-permute-done((f32[4,2,64,128]{3,2,1,0:T(8,128)S(1)}, f32[4,2,64,128]{3,2,1,0:T(8,128)S(1)}, u32[]{:S(2)}, u32[]{:S(2)}) %collective-permute-start.18) | collective-permute-done | bytes 262176 | tf_op jit(solution)/shard_map/ppermute | solution.py:462
  119.8 3.4 %collective-permute-done.20 = f32[4,2,64,128]{3,2,1,0:T(8,128)S(1)} collective-permute-done((f32[4,2,64,128]{3,2,1,0:T(8,128)S(1)}, f32[4,2,64,128]{3,2,1,0:T(8,128)S(1)}, u32[]{:S(2)}, u32[]{:S(2)}) %collective-permute-start.20) | collective-permute-done | bytes 262176 | tf_op jit(solution)/shard_map/ppermute | solution.py:462
  124.9 4.1 %all-to-all-start = ((f32[4,2,2,64,128]{4,3,2,1,0:T(8,128)}), f32[4,2,2,64,128]{4,3,2,1,0:T(8,128)S(1)}, u32[]{:S(2)}, u32[]{:S(2)}) async-start(f32[4,2,2,64,128]{4,3,2,1,0:T(8,128)} %pad_maximum_fusion.1), calls=%async_computation | async-start | bytes 1048576 | tf_op jit(solution)/shard_map/all_to_all | solution.py:491
  129.0 6.4 %collective-permute-done.12.refs_3_ = f32[2,64,1024]{2,1,0:T(8,128)S(1)} collective-permute-done((f32[2,64,1024]{2,1,0:T(8,128)S(1)}, f32[2,64,1024]{2,1,0:T(8,128)S(1)}, u32[]{:S(2)}, u32[]{:S(2)}) %collective-permute-start.12) | collective-permute-done | bytes 524320 | tf_op jit(solution)/shard_map/ppermute | solution.py:462
  136.9 3.1 %all-to-all-done.both_ref = f32[4,2,2,64,128]{4,3,2,1,0:T(8,128)S(1)} async-done(((f32[4,2,2,64,128]{4,3,2,1,0:T(8,128)}), f32[4,2,2,64,128]{4,3,2,1,0:T(8,128)S(1)}, u32[]{:S(2)}, u32[]{:S(2)}) %all-to-all-start) | async-done | bytes 524320 | tf_op jit(solution)/shard_map/all_to_all | solution.py:491
  (50 shorter events, 21.4 us)
Async XLA Ops:
  2.4 24.7 %copy-start = (bf16[1,2,64,4096]{3,2,1,0:T(8,128)(2,1)S(1)}, bf16[1,2,64,4096]{3,2,1,0:T(8,128)(2,1)}, u32[]{:S(2)}) copy-start(bf16[1,2,64,4096]{3,2,1,0:T(8,128)(2,1)} %refs_1_.3) | copy-start | bytes 3145732
  2.5 24.7 %copy-start.1 = (bf16[1,2,64,4096]{3,2,1,0:T(8,128)(2,1)S(1)}, bf16[1,2,64,4096]{3,2,1,0:T(8,128)(2,1)}, u32[]{:S(2)}) copy-start(bf16[1,2,64,4096]{3,2,1,0:T(8,128)(2,1)} %refs_2_.3) | copy-start | bytes 3145732
  2.5 5.5 %collective-permute-start = (bf16[2,2,64,128]{3,2,1,0:T(8,128)(2,1)S(1)}, bf16[2,2,64,128]{3,2,1,0:T(8,128)(2,1)S(1)}, u32[]{:S(2)}, u32[]{:S(2)}) collective-permute-start(bf16[2,2,64,128]{3,2,1,0:T(8,128)(2,1)S(1)} %get-tuple-element.27), channel_id=1, source_target_pairs={{0,32},{4,36},{8,40},{12,44},{16,48},{20,52},{24,56},{28,60},{32,6... | collective-permute-start | bytes 196616 | tf_op jit(solution)/shard_map/ppermute | solution.py:462
  4.3 4.4 %collective-permute-start.1 = (bf16[2,2,64,128]{3,2,1,0:T(8,128)(2,1)S(1)}, bf16[2,2,64,128]{3,2,1,0:T(8,128)(2,1)S(1)}, u32[]{:S(2)}, u32[]{:S(2)}) collective-permute-start(bf16[2,2,64,128]{3,2,1,0:T(8,128)(2,1)S(1)} %get-tuple-element.28), channel_id=1, source_target_pairs={{0,96},{4,100},{8,104},{12,108},{16,112},{20,116},{24,120},{28,124... | collective-permute-start | bytes 196616 | tf_op jit(solution)/shard_map/ppermute | solution.py:462
  5.8 5.8 %collective-permute-start.2 = (bf16[2,2,64,128]{3,2,1,0:T(8,128)(2,1)S(1)}, bf16[2,2,64,128]{3,2,1,0:T(8,128)(2,1)S(1)}, u32[]{:S(2)}, u32[]{:S(2)}) collective-permute-start(bf16[2,2,64,128]{3,2,1,0:T(8,128)(2,1)S(1)} %get-tuple-element.29), channel_id=1, source_target_pairs={{0,64},{4,68},{8,72},{12,76},{16,80},{20,84},{24,88},{28,92},{32,9... | collective-permute-start | bytes 196616 | tf_op jit(solution)/shard_map/ppermute | solution.py:462
  11.6 11.2 %collective-permute-start.4 = (bf16[4,2,2,64,128]{4,3,2,1,0:T(8,128)(2,1)S(1)}, bf16[4,2,2,64,128]{4,3,2,1,0:T(8,128)(2,1)S(1)}, u32[]{:S(2)}, u32[]{:S(2)}) collective-permute-start(bf16[4,2,2,64,128]{4,3,2,1,0:T(8,128)(2,1)S(1)} %get-tuple-element.58), channel_id=1, source_target_pairs={{0,16},{4,20},{8,24},{12,28},{16,0},{20,4},{24,8},{28,12},{32,48},... | collective-permute-start | bytes 786440 | tf_op jit(solution)/shard_map/ppermute | solution.py:462
  15.7 10.4 %collective-permute-start.3 = (bf16[4,2,2,64,128]{4,3,2,1,0:T(8,128)(2,1)S(1)}, bf16[4,2,2,64,128]{4,3,2,1,0:T(8,128)(2,1)S(1)}, u32[]{:S(2)}, u32[]{:S(2)}) collective-permute-start(bf16[4,2,2,64,128]{4,3,2,1,0:T(8,128)(2,1)S(1)} %get-tuple-element.58), channel_id=1, source_target_pairs={{0,8},{4,12},{8,16},{12,20},{16,24},{20,28},{24,0},{28,4},{32,40},... | collective-permute-start | bytes 786440 | tf_op jit(solution)/shard_map/ppermute | solution.py:462
  16.7 10.1 %collective-permute-start.5 = (bf16[4,2,2,64,128]{4,3,2,1,0:T(8,128)(2,1)S(1)}, bf16[4,2,2,64,128]{4,3,2,1,0:T(8,128)(2,1)S(1)}, u32[]{:S(2)}, u32[]{:S(2)}) collective-permute-start(bf16[4,2,2,64,128]{4,3,2,1,0:T(8,128)(2,1)S(1)} %get-tuple-element.58), channel_id=1, source_target_pairs={{0,24},{4,28},{8,0},{12,4},{16,8},{20,12},{24,16},{28,20},{32,56},... | collective-permute-start | bytes 786440 | tf_op jit(solution)/shard_map/ppermute | solution.py:462
  26.9 7.7 %collective-permute-start.6 = (bf16[4,4,2,2,64,128]{5,4,3,2,1,0:T(8,128)(2,1)S(1)}, bf16[4,4,2,2,64,128]{5,4,3,2,1,0:T(8,128)(2,1)}, u32[]{:S(2)}, u32[]{:S(2)}) collective-permute-start(bf16[4,4,2,2,64,128]{5,4,3,2,1,0:T(8,128)(2,1)S(1)} %pad_maximum_fusion.kv_own), channel_id=1, source_target_pairs={{0,4},{4,0},{8,12},{12,8},{16,20},{20,16},{24,28},{28,24},{32,36},... | collective-permute-start | bytes 3145736 | tf_op jit(solution)/shard_map/ppermute | solution.py:462
  30.1 17.1 %collective-permute-start.7 = (bf16[2,64,2176]{2,1,0:T(8,128)(2,1)S(1)}, bf16[2,64,2176]{2,1,0:T(8,128)(2,1)S(1)}, u32[]{:S(2)}, u32[]{:S(2)}) collective-permute-start(bf16[2,64,2176]{2,1,0:T(8,128)(2,1)S(1)} %get-tuple-element.31), channel_id=1, source_target_pairs={{0,32},{4,36},{8,40},{12,44},{16,48},{20,52},{24,56},{28,60},{32,6... | collective-permute-start | bytes 1671176 | tf_op jit(solution)/shard_map/ppermute | solution.py:462
  30.7 27.0 %collective-permute-start.8 = (bf16[2,64,2176]{2,1,0:T(8,128)(2,1)S(1)}, bf16[2,64,2176]{2,1,0:T(8,128)(2,1)S(1)}, u32[]{:S(2)}, u32[]{:S(2)}) collective-permute-start(bf16[2,64,2176]{2,1,0:T(8,128)(2,1)S(1)} %get-tuple-element.32), channel_id=1, source_target_pairs={{0,96},{4,100},{8,104},{12,108},{16,112},{20,116},{24,120},{28,124... | collective-permute-start | bytes 1671176 | tf_op jit(solution)/shard_map/ppermute | solution.py:462
  33.4 25.0 %collective-permute-start.9 = (bf16[2,64,2176]{2,1,0:T(8,128)(2,1)S(1)}, bf16[2,64,2176]{2,1,0:T(8,128)(2,1)S(1)}, u32[]{:S(2)}, u32[]{:S(2)}) collective-permute-start(bf16[2,64,2176]{2,1,0:T(8,128)(2,1)S(1)} %get-tuple-element.37), channel_id=1, source_target_pairs={{0,64},{4,68},{8,72},{12,76},{16,80},{20,84},{24,88},{28,92},{32,9... | collective-permute-start | bytes 1671176 | tf_op jit(solution)/shard_map/ppermute | solution.py:462
  93.7 2.7 %collective-permute-start.13 = (f32[4,4,2,64,128]{4,3,2,1,0:T(8,128)S(1)}, f32[4,4,2,64,128]{4,3,2,1,0:T(8,128)S(1)}, u32[]{:S(2)}, u32[]{:S(2)}) collective-permute-start(f32[4,4,2,64,128]{4,3,2,1,0:T(8,128)S(1)} %get-tuple-element.44), channel_id=1, source_target_pairs={{0,4},{4,0},{8,12},{12,8},{16,20},{20,16},{24,28},{28,24},{32,36},... | collective-permute-start | bytes 3145736 | tf_op jit(solution)/shard_map/ppermute | solution.py:462
  93.8 9.1 %collective-permute-start.17 = (f32[4,4,2,64,128]{4,3,2,1,0:T(8,128)S(1)}, f32[4,4,2,64,128]{4,3,2,1,0:T(8,128)S(1)}, u32[]{:S(2)}, u32[]{:S(2)}) collective-permute-start(f32[4,4,2,64,128]{4,3,2,1,0:T(8,128)S(1)} %get-tuple-element.46), channel_id=1, source_target_pairs={{0,4},{4,0},{8,12},{12,8},{16,20},{20,16},{24,28},{28,24},{32,36},... | collective-permute-start | bytes 3145736 | tf_op jit(solution)/shard_map/ppermute | solution.py:462
  96.6 9.6 %collective-permute-start.14 = (f32[4,2,64,128]{3,2,1,0:T(8,128)S(1)}, f32[4,2,64,128]{3,2,1,0:T(8,128)S(1)}, u32[]{:S(2)}, u32[]{:S(2)}) collective-permute-start(f32[4,2,64,128]{3,2,1,0:T(8,128)S(1)} %get-tuple-element.49), channel_id=1, source_target_pairs={{0,8},{4,12},{8,16},{12,20},{16,24},{20,28},{24,0},{28,4},{32,40},... | collective-permute-start | bytes 786440 | tf_op jit(solution)/shard_map/ppermute | solution.py:462
  97.7 13.7 %collective-permute-start.16 = (f32[4,2,64,128]{3,2,1,0:T(8,128)S(1)}, f32[4,2,64,128]{3,2,1,0:T(8,128)S(1)}, u32[]{:S(2)}, u32[]{:S(2)}) collective-permute-start(f32[4,2,64,128]{3,2,1,0:T(8,128)S(1)} %get-tuple-element.50), channel_id=1, source_target_pairs={{0,24},{4,28},{8,0},{12,4},{16,8},{20,12},{24,16},{28,20},{32,56},... | collective-permute-start | bytes 786440 | tf_op jit(solution)/shard_map/ppermute | solution.py:462
  99.9 15.5 %collective-permute-start.15 = (f32[4,2,64,128]{3,2,1,0:T(8,128)S(1)}, f32[4,2,64,128]{3,2,1,0:T(8,128)S(1)}, u32[]{:S(2)}, u32[]{:S(2)}) collective-permute-start(f32[4,2,64,128]{3,2,1,0:T(8,128)S(1)} %get-tuple-element.51), channel_id=1, source_target_pairs={{0,16},{4,20},{8,24},{12,28},{16,0},{20,4},{24,8},{28,12},{32,48},... | collective-permute-start | bytes 786440 | tf_op jit(solution)/shard_map/ppermute | solution.py:462
  101.9 27.2 %collective-permute-start.11 = (f32[2,64,1024]{2,1,0:T(8,128)}, f32[2,64,1024]{2,1,0:T(8,128)S(1)}, u32[]{:S(2)}, u32[]{:S(2)}) collective-permute-start(f32[2,64,1024]{2,1,0:T(8,128)} %get-tuple-element.55), channel_id=1, source_target_pairs={{0,32},{4,36},{8,40},{12,44},{16,48},{20,52},{24,56},{28,60},{32,6... | collective-permute-start | bytes 1572872 | tf_op jit(solution)/shard_map/ppermute | solution.py:462
  102.9 26.1 %collective-permute-start.10 = (f32[2,64,1024]{2,1,0:T(8,128)}, f32[2,64,1024]{2,1,0:T(8,128)S(1)}, u32[]{:S(2)}, u32[]{:S(2)}) collective-permute-start(f32[2,64,1024]{2,1,0:T(8,128)} %get-tuple-element.56), channel_id=1, source_target_pairs={{0,96},{4,100},{8,104},{12,108},{16,112},{20,116},{24,120},{28,124... | collective-permute-start | bytes 1572872 | tf_op jit(solution)/shard_map/ppermute | solution.py:462
  106.2 12.9 %collective-permute-start.18 = (f32[4,2,64,128]{3,2,1,0:T(8,128)S(1)}, f32[4,2,64,128]{3,2,1,0:T(8,128)S(1)}, u32[]{:S(2)}, u32[]{:S(2)}) collective-permute-start(f32[4,2,64,128]{3,2,1,0:T(8,128)S(1)} %get-tuple-element.52), channel_id=1, source_target_pairs={{0,8},{4,12},{8,16},{12,20},{16,24},{20,28},{24,0},{28,4},{32,40},... | collective-permute-start | bytes 786440 | tf_op jit(solution)/shard_map/ppermute | solution.py:462
  111.4 11.8 %collective-permute-start.20 = (f32[4,2,64,128]{3,2,1,0:T(8,128)S(1)}, f32[4,2,64,128]{3,2,1,0:T(8,128)S(1)}, u32[]{:S(2)}, u32[]{:S(2)}) collective-permute-start(f32[4,2,64,128]{3,2,1,0:T(8,128)S(1)} %get-tuple-element.53), channel_id=1, source_target_pairs={{0,24},{4,28},{8,0},{12,4},{16,8},{20,12},{24,16},{28,20},{32,56},... | collective-permute-start | bytes 786440 | tf_op jit(solution)/shard_map/ppermute | solution.py:462
  115.4 8.6 %collective-permute-start.19 = (f32[4,2,64,128]{3,2,1,0:T(8,128)S(1)}, f32[4,2,64,128]{3,2,1,0:T(8,128)S(1)}, u32[]{:S(2)}, u32[]{:S(2)}) collective-permute-start(f32[4,2,64,128]{3,2,1,0:T(8,128)S(1)} %get-tuple-element.54), channel_id=1, source_target_pairs={{0,16},{4,20},{8,24},{12,28},{16,0},{20,4},{24,8},{28,12},{32,48},... | collective-permute-start | bytes 786440 | tf_op jit(solution)/shard_map/ppermute | solution.py:462
  119.1 16.3 %collective-permute-start.12 = (f32[2,64,1024]{2,1,0:T(8,128)S(1)}, f32[2,64,1024]{2,1,0:T(8,128)S(1)}, u32[]{:S(2)}, u32[]{:S(2)}) collective-permute-start(f32[2,64,1024]{2,1,0:T(8,128)S(1)} %get-tuple-element.42), channel_id=1, source_target_pairs={{0,64},{4,68},{8,72},{12,76},{16,80},{20,84},{24,88},{28,92},{32,9... | collective-permute-start | bytes 1572872 | tf_op jit(solution)/shard_map/ppermute | solution.py:462
  124.9 15.1 %all-to-all-start = ((f32[4,2,2,64,128]{4,3,2,1,0:T(8,128)}), f32[4,2,2,64,128]{4,3,2,1,0:T(8,128)S(1)}, u32[]{:S(2)}, u32[]{:S(2)}) async-start(f32[4,2,2,64,128]{4,3,2,1,0:T(8,128)} %pad_maximum_fusion.1), calls=%async_computation | async-start | bytes 1048576 | tf_op jit(solution)/shard_map/all_to_all | solution.py:491
  (4 other events, 27.6 us)
